TPU v7x, 32 devices: a whole 2x2x4 slice. The times are simulated.
32 devices in a mesh: dp: 8 (over z, y), tensor: 4 (over x, core).
Axes of the slice: x: 2, y: 2, z: 4, core: 2. Of those that a mesh axis runs over, the one named last changes fastest.
Arguments:
- hidden: bfloat16 [4096, 5120], P('dp'), may hold values from -48 to 48
- head_weight: bfloat16 [5120, 4096], P(None, 'tensor'), may hold values from -0.069877124 to 0.069877124
- token_ids: int32 [4096], P('dp'), may hold values from 0 to 4095
- old_logprob: float32 [4096], P('dp'), may hold values from -12.5 to 0.3
- rewards: int32 [64], P('dp'), may hold values from 0 to 1, as said below
- lengths: int32 [64], P('dp'), may hold values from 1 to 64, as said below
- group_ids: int32 [64], P('dp'), may hold values from 0 to 3, as said below
- loss_scale: float32 [], replicated, may hold values from 4096 to 16384
Outputs:
- loss: float32 [], replicated
- grad_hidden: float32 [4096, 5120], P('dp', 'tensor')
- grad_weight: float32 [5120, 4096], P('dp', 'tensor')
Inputs may be any that keep to these rules, and one draw needn't show every extreme that they name: `group_ids`: each group number names exactly 16 rollouts. `rewards`: some group holds both a 0 and a 1. `lengths`: some index of dp holds only rollouts of length 64 whose prompts hold both a 0 and a 1.
All inputs are finite; a program needn't handle non-finite values.
Results may differ from a plain program's by a relative error of at most 0.003.
Values may be sent and summed in bfloat16 or wider, within the bound.
A program may use at most 192 MiB of HBM per device.

v0:
```python
import jax
import jax.numpy as jnp
from jax import lax
from jax.sharding import PartitionSpec as P

GROUP = 16
clip_low = 0.2
clip_high = 0.28


def contract_rows(first_operand, second_operand):
    return lax.dot_general(
        first_operand, second_operand, (((0,), (0,)), ((), ())), preferred_element_type=jnp.float32
    )


def contract_cols(first_operand, second_operand):
    return lax.dot_general(
        first_operand, second_operand, (((1,), (1,)), ((), ())), preferred_element_type=jnp.float32
    )


def run_blocks(block_fn, initial):
    return block_fn(0, initial)


def group_terms(member, group_wins, reward_float):
    group_alive = jnp.logical_and(group_wins > 0.5, group_wins < GROUP - 0.5).astype(jnp.float32)
    center = group_wins / GROUP
    spread = jnp.where(group_alive > 0.5, jnp.sqrt(group_wins * (GROUP - group_wins)) / GROUP, 1.0)
    roll_alive = jnp.sum(member * group_alive[None, :], axis=1)
    roll_center = jnp.sum(member * center[None, :], axis=1)
    roll_spread = jnp.sum(member * spread[None, :], axis=1)
    advantage = roll_alive * (reward_float - roll_center) / roll_spread
    return (group_alive, roll_alive, advantage)


def policy_terms(log_prob, old_rows, adv_rows, weight_rows, factor):
    prob_ratio = jnp.exp(log_prob - old_rows)
    clipped = jnp.clip(prob_ratio, 1.0 - clip_low, 1.0 + clip_high)
    token_loss = -jnp.minimum(prob_ratio * adv_rows, clipped * adv_rows)
    active = prob_ratio * adv_rows <= clipped * adv_rows
    coefficient = jnp.where(active, -adv_rows * prob_ratio, 0.0) * weight_rows * factor
    return (token_loss, coefficient)


def shards(hidden, head_weight, token_ids, old_logprob, rewards, lengths, group_ids, loss_scale):
    row_count, model_width = hidden.shape
    roll_count = rewards.shape[0]
    response = row_count // roll_count
    vocab_part = head_weight.shape[1]
    data_size = lax.axis_size("dp")
    group_count = roll_count * data_size // GROUP
    member = (group_ids[:, None] == jnp.arange(group_count, dtype=jnp.int32)[None, :]).astype(
        jnp.float32
    )
    reward_float = rewards.astype(jnp.float32)
    length_float = lengths.astype(jnp.float32)
    local_wins = jnp.sum(member * reward_float[:, None], axis=0)
    group_wins = lax.psum(local_wins, "dp")
    group_alive, roll_alive, advantage = group_terms(member, group_wins, reward_float)
    token_count = lax.psum(jnp.sum(roll_alive * length_float), "dp")
    divisor = jnp.maximum(token_count, 1.0)
    factor = loss_scale / divisor
    position = jnp.arange(response, dtype=jnp.int32)
    inside = (position[None, :] < lengths[:, None]).astype(jnp.float32)
    token_weight = (roll_alive[:, None] * inside).reshape(row_count)
    token_adv = jnp.broadcast_to(advantage[:, None], (roll_count, response)).reshape(row_count)

    def logit_block(block_index, current):
        block_logits = jnp.dot(hidden, head_weight, preferred_element_type=jnp.float32)
        return block_logits

    logits = run_blocks(logit_block, jnp.zeros((row_count, vocab_part), jnp.float32))
    row_top = lax.pmax(jnp.max(logits, axis=1), "tensor")
    shifted = jnp.exp(logits - row_top[:, None])
    column = (
        jnp.arange(vocab_part, dtype=jnp.int32)[None, :] + lax.axis_index("tensor") * vocab_part
    )
    is_target = column == token_ids[:, None]
    row_total, target = lax.psum(
        (jnp.sum(shifted, axis=1), jnp.sum(jnp.where(is_target, logits, 0.0), axis=1)), "tensor"
    )
    softmax_rows = shifted / row_total[:, None]
    log_prob = target - row_top - jnp.log(row_total)
    token_loss, coefficient = policy_terms(log_prob, old_logprob, token_adv, token_weight, factor)
    logit_grad = (coefficient[:, None] * (is_target.astype(jnp.float32) - softmax_rows)).astype(
        jnp.bfloat16
    )

    def grad_block(block_index, current):
        return contract_cols(logit_grad, head_weight)

    grad_part = run_blocks(grad_block, jnp.zeros((row_count, model_width), jnp.float32))
    columns = lax.all_to_all(hidden, "dp", split_axis=1, concat_axis=0, tiled=True)
    grad_weight = contract_rows(columns, lax.all_gather(logit_grad, "dp", axis=0, tiled=True))
    grad_cols = lax.psum_scatter(grad_part, "tensor", scatter_dimension=1, tiled=True)
    loss_total = lax.psum(jnp.sum(token_weight * token_loss), "dp")
    return (loss_total / divisor, grad_cols, grad_weight)


def solution(mesh):
    return jax.shard_map(
        shards,
        mesh=mesh,
        in_specs=(
            P("dp", None),
            P(None, "tensor"),
            P("dp"),
            P("dp"),
            P("dp"),
            P("dp"),
            P("dp"),
            P(),
        ),
        out_specs=(P(), P("dp", "tensor"), P("dp", "tensor")),
        check_vma=False,
    )
```

profile of v0, /device:TPU:4, one launch (start us, length us, event | category | flops | bytes accessed | tf_op | source)
XLA Modules:
  0.0 332.5 jit_solution(15351003358301694592)
XLA Ops:
  8.0 0.0 all-gather.2.cloned.1.call-start
  8.0 0.7 convert_element_type.17
  8.7 0.8 select_reduce_fusion.3
  9.5 18.0 %psum.35 = f32[4]{0:T(128)S(1)} all-reduce(f32[4]{0:T(128)S(1)} %select_reduce_fusion.3), channel_id=1, replica_groups=mesh['dp'=8,'tensor'=4] {'dp'}, use_global_device_ids=true, to_apply=%region_1.0 | all-reduce | flops 4 | bytes 32 | tf_op jit(solution)/shard_map/psum | solution.py:60
  28.1 0.7 select_reduce_fusion.1
  28.9 0.7 fusion.5
  29.6 1.3 multiply_reduce_fusion.1
  30.9 0.1 broadcast_in_dim.12
  30.9 0.1 reshape.36
  31.0 0.1 mul.91
  31.1 0.0 copy-start
  31.1 0.0 copy-start.1
  31.1 10.0 %fusion.8 = (f32[512]{0:T(512)S(1)}, f32[512,1024]{1,0:T(8,128)S(1)}) fusion(bf16[512,5120]{1,0:T(8,128)(2,1)} %param.8, bf16[5120,1024]{1,0:T(8,128)(2,1)} %param.9), kind=kOutput, calls=%fused_computation.29 | convolution fusion | flops 5369232896 | bytes 17827840 | tf_op jit(solution)/shard_map/dot_general | solution.py:71
  41.1 5.7 %pmax.7 = f32[512]{0:T(512)S(1)} all-reduce(f32[512]{0:T(512)S(1)} %get-tuple-element.30), channel_id=1, replica_groups=mesh['dp'=8,'tensor'=4] {'tensor'}, use_global_device_ids=true, to_apply=%region_6.7 | all-reduce | flops 512 | bytes 4096 | tf_op jit(solution)/shard_map/pmax | solution.py:75
  46.8 0.0 copy-done
  46.8 0.7 fusion
  47.5 6.6 %all-reduce.1 = (f32[512]{0:T(512)S(1)}, f32[512]{0:T(512)S(1)}) all-reduce(f32[512]{0:T(512)S(1)} %get-tuple-element.16, f32[512]{0:T(512)S(1)} %get-tuple-element.15), channel_id=1, replica_groups=mesh['dp'=8,'tensor'=4] {'tensor'}, use_global_device_ids=true, to_apply=%region_8.9 | all-reduce | flops 1024 | bytes 8192 | tf_op jit(solution)/shard_map/psum | solution.py:81
  54.1 0.0 copy-done.1
  54.1 0.6 multiply_reduce_fusion
  54.7 22.0 %all-reduce = (f32[]{:T(128)}, f32[]{:T(128)}) all-reduce(f32[]{:T(128)} %get-tuple-element.24, f32[]{:T(128)} %get-tuple-element.26), channel_id=1, replica_groups=mesh['dp'=8,'tensor'=4] {'dp'}, use_global_device_ids=true, to_apply=%region_12.13 | all-reduce | flops 2 | bytes 16 | tf_op jit(solution)/shard_map/psum | solution.py:98
  77.4 1.6 fusion.3
  79.1 0.0 all-gather.2.cloned.1.call-update
  79.1 0.0 reduce-scatter.2.cloned.1.call-start
  79.2 10.9 %fusion.9 = f32[512,5120]{1,0:T(8,128)} fusion(bf16[512,1024]{1,0:T(8,128)(2,1)} %fusion.3, bf16[5120,1024]{1,0:T(8,128)(2,1)} %param.9), kind=kOutput, calls=%fused_computation.30 | convolution fusion | flops 5368709120 | bytes 22020096 | tf_op jit(solution)/shard_map/dot_general | solution.py:18
  90.1 0.0 reduce-scatter.2.cloned.1.call-update
  90.1 8.2 %copy.16 = bf16[512,5120]{0,1:T(8,128)(2,1)} copy(bf16[512,5120]{1,0:T(8,128)(2,1)} %param.8) | data formatting | bytes 10485760 | tf_op args[0]
  98.3 4.8 %all-to-all-start = ((bf16[512,8,640]{0,2,1:T(8,128)(2,1)}), bf16[512,8,640]{0,2,1:T(8,128)(2,1)}, u32[]{:S(2)}, u32[]{:S(2)}) async-start(bf16[512,8,640]{0,2,1:T(8,128)(2,1)} %bitcast.11), calls=%async_computation.1 | async-start | bytes 10485760 | tf_op jit(solution)/shard_map/all_to_all | solution.py:95
  103.8 199.4 %all-to-all-done = bf16[512,8,640]{0,2,1:T(8,128)(2,1)} async-done(((bf16[512,8,640]{0,2,1:T(8,128)(2,1)}), bf16[512,8,640]{0,2,1:T(8,128)(2,1)}, u32[]{:S(2)}, u32[]{:S(2)}) %all-to-all-start) | async-done | bytes 5242912 | tf_op jit(solution)/shard_map/all_to_all | solution.py:95
  303.2 7.9 %copy.17 = bf16[8,512,640]{2,1,0:T(8,128)(2,1)} copy(bf16[8,512,640]{1,2,0:T(8,128)(2,1)} %bitcast.1) | data formatting | bytes 10485760 | tf_op jit(solution)/shard_map/all_to_all | solution.py:95
  311.1 0.0 all-gather.2.cloned.1.call-done
  311.1 10.7 %convolution_bitcast_fusion = f32[640,1024]{0,1:T(8,128)S(1)} fusion(bf16[4096,1024]{1,0:T(8,128)(2,1)} %all-gather.2.cloned.1.call-done, bf16[4096,640]{1,0:T(8,128)(2,1)} %bitcast.12), kind=kOutput, calls=%fused_computation.8 | convolution fusion | flops 5368709120 | bytes 16252928 | tf_op jit(solution)/shard_map/dot_general | solution.py:12
  321.8 2.1 copy.18
  (5 shorter events, 0.0 us)
Async XLA Ops:
  8.0 303.1 %all-gather.2.cloned.1.call-start = ((), (), s32[]{:S(2)}) async-start(), calls=%async_computation.3 | async-start | bytes 9437184 | tf_op jit(solution)/shard_map/all_gather | solution.py:96
  31.1 15.7 %copy-start = (s32[512]{0:T(512)S(1)}, s32[512]{0:T(512)}, u32[]{:S(2)}) copy-start(s32[512]{0:T(512)} %param.10) | copy-start | bytes 6148
  31.1 23.0 %copy-start.1 = (f32[512]{0:T(512)S(1)}, f32[512]{0:T(512)}, u32[]{:S(2)}) copy-start(f32[512]{0:T(512)} %param.11) | copy-start | bytes 6148
  79.1 244.8 %reduce-scatter.2.cloned.1.call-start = ((), (), s32[]{:S(2)}) async-start(), calls=%async_computation.2 | async-start | bytes 13107200 | tf_op jit(solution)/shard_map/reduce_scatter | solution.py:97
  98.3 204.9 %all-to-all-start = ((bf16[512,8,640]{0,2,1:T(8,128)(2,1)}), bf16[512,8,640]{0,2,1:T(8,128)(2,1)}, u32[]{:S(2)}, u32[]{:S(2)}) async-start(bf16[512,8,640]{0,2,1:T(8,128)(2,1)} %bitcast.11), calls=%async_computation.1 | async-start | bytes 10485760 | tf_op jit(solution)/shard_map/all_to_all | solution.py:95
Sparse Core Ops, SparseCore 0:
  79.2 219.8 all-gather.1
Sparse Core Ops, SparseCore 1:
  90.2 81.7 reduce-scatter.1
where the time goes:
time: 333 us; the launch traced here: 332 us
  waiting for transfers between devices  199 us (60%)
  blocking collectives  52.3 us (16%)
  matrix products  31.7 us (10%)
  between operations  18.7 us (6%)
  local copies, waits for them, and re-layouts  18.4 us (6%)
  other arithmetic  7.13 us (2%)
  starting transfers between devices  4.89 us (1%)
    all_to_all x1, waiting for transfers between devices, shards(): lax.all_to_all(hidden, 'dp', split_axis=1, concat_axis=0, tiled=True)  199 us
    psum x1, blocking collectives, shards(): loss_total = lax.psum(jnp.sum(token_weight * token_loss), 'dp')  22 us
    psum x1, blocking collectives, shards(): group_wins = lax.psum(local_wins, 'dp')  18 us
    dot_general x1, matrix products, contract_cols(): lax.dot_general(first_operand, second_operand, (((1,), (1,)), ((), ())),...  10.9 us
    dot_general x1, matrix products, contract_rows(): lax.dot_general(first_operand, second_operand, (((0,), (0,)), ((), ())),...  10.7 us
    unnamed x6, local copies, waits for them, and re-layouts  10.3 us
    dot_general x1, matrix products, logit_block(): jnp.dot(hidden, head_weight, preferred_element_type=jnp.float32)  10 us
    all_to_all x1, local copies, waits for them, and re-layouts, shards(): lax.all_to_all(hidden, 'dp', split_axis=1, concat_axis=0, tiled=True)  7.87 us
  transfers between devices with their start and end apart: 3, of which 1 were waited for; matrix products, arithmetic and copies ran while one was open for 12% of the time, Pallas kernels for 0%

commit v1 on v0

--- a/solution.py
+++ b/solution.py
@@ -92,7 +92,10 @@
         return contract_cols(logit_grad, head_weight)
 
     grad_part = run_blocks(grad_block, jnp.zeros((row_count, model_width), jnp.float32))
-    columns = lax.all_to_all(hidden, "dp", split_axis=1, concat_axis=0, tiled=True)
+    columns = jnp.concatenate(
+        lax.all_to_all(jnp.stack(jnp.split(hidden, lax.axis_size("dp"), axis=1)), "dp", 0, 0),
+        axis=0,
+    )
     grad_weight = contract_rows(columns, lax.all_gather(logit_grad, "dp", axis=0, tiled=True))
     grad_cols = lax.psum_scatter(grad_part, "tensor", scatter_dimension=1, tiled=True)
     loss_total = lax.psum(jnp.sum(token_weight * token_loss), "dp")

time: 333 us -> 325 us (0.976)
  waiting for transfers between devices: 199 us -> 191 us
    all_to_all x1, waiting for transfers between devices: 199 us -> 191 us  [shards(): lax.all_to_all(jnp.stack(jnp.split(hidden, lax.axis_size('dp'), axis=1)),...]
    all_to_all x1 -> x0, local copies, waits for them, and re-layouts: 7.87 us -> none  [shards(): lax.all_to_all(hidden, 'dp', split_axis=1, concat_axis=0, tiled=True)]
    unnamed x6 -> x11, local copies, waits for them, and re-layouts: 10.3 us -> 14.7 us
where the time goes in v1:
time: 325 us; the launch traced here: 322 us
  waiting for transfers between devices  191 us (59%)
  blocking collectives  52.3 us (16%)
  matrix products  31.6 us (10%)
  between operations  18.7 us (6%)
  local copies, waits for them, and re-layouts  17 us (5%)
  other arithmetic  7.14 us (2%)
  starting transfers between devices  4.69 us (1%)
    all_to_all x1, waiting for transfers between devices, shards(): lax.all_to_all(jnp.stack(jnp.split(hidden, lax.axis_size('dp'), axis=1)),...  191 us
    psum x1, blocking collectives, shards(): loss_total = lax.psum(jnp.sum(token_weight * token_loss), 'dp')  22 us
    psum x1, blocking collectives, shards(): group_wins = lax.psum(local_wins, 'dp')  18 us
    unnamed x11, local copies, waits for them, and re-layouts  14.7 us
    dot_general x1, matrix products, contract_cols(): lax.dot_general(first_operand, second_operand, (((1,), (1,)), ((), ())),...  10.9 us
    dot_general x1, matrix products, contract_rows(): lax.dot_general(first_operand, second_operand, (((0,), (0,)), ((), ())),...  10.6 us
    dot_general x1, matrix products, logit_block(): jnp.dot(hidden, head_weight, preferred_element_type=jnp.float32)  10 us
    psum x1, blocking collectives, shards(): lax.psum((jnp.sum(shifted, axis=1), jnp.sum(jnp.where(is_target, logits,...  6.62 us
  transfers between devices with their start and end apart: 3, of which 1 were waited for; matrix products, arithmetic and copies ran while one was open for 12% of the time, Pallas kernels for 0%

profile of v1, /device:TPU:4, one launch (start us, length us, event | category | flops | bytes accessed | tf_op | source)
XLA Modules:
  0.0 322.5 jit_solution(18044664308599387839)
XLA Ops:
  8.0 0.0 all-gather.2.cloned.1.call-start
  8.0 0.7 convert_element_type.17
  8.7 0.8 select_reduce_fusion.3
  9.5 18.0 %psum.35 = f32[4]{0:T(128)S(1)} all-reduce(f32[4]{0:T(128)S(1)} %select_reduce_fusion.3), channel_id=1, replica_groups=mesh['dp'=8,'tensor'=4] {'dp'}, use_global_device_ids=true, to_apply=%region_1.0 | all-reduce | flops 4 | bytes 32 | tf_op jit(solution)/shard_map/psum | solution.py:60
  27.5 0.7 select_reduce_fusion.1
  28.2 0.7 fusion.5
  28.9 0.1 mul.91
  29.0 1.3 multiply_reduce_fusion.1
  30.3 0.1 broadcast_in_dim.12
  30.4 0.1 reshape.36
  30.4 10.0 %fusion.8 = (f32[512]{0:T(512)S(1)}, f32[512,1024]{1,0:T(8,128)S(1)}) fusion(bf16[512,5120]{1,0:T(8,128)(2,1)} %param.8, bf16[5120,1024]{1,0:T(8,128)(2,1)} %param.9), kind=kOutput, calls=%fused_computation.36 | convolution fusion | flops 5369232896 | bytes 17827840 | tf_op jit(solution)/shard_map/dot_general | solution.py:71
  40.5 5.7 %pmax.7 = f32[512]{0:T(512)S(1)} all-reduce(f32[512]{0:T(512)S(1)} %get-tuple-element.18), channel_id=1, replica_groups=mesh['dp'=8,'tensor'=4] {'tensor'}, use_global_device_ids=true, to_apply=%region_6.7 | all-reduce | flops 512 | bytes 4096 | tf_op jit(solution)/shard_map/pmax | solution.py:75
  46.8 0.7 fusion
  47.5 6.6 %all-reduce.1 = (f32[512]{0:T(512)S(1)}, f32[512]{0:T(512)S(1)}) all-reduce(f32[512]{0:T(512)S(1)} %get-tuple-element.4, f32[512]{0:T(512)S(1)} %get-tuple-element.3), channel_id=1, replica_groups=mesh['dp'=8,'tensor'=4] {'tensor'}, use_global_device_ids=true, to_apply=%region_8.9 | all-reduce | flops 1024 | bytes 8192 | tf_op jit(solution)/shard_map/psum | solution.py:81
  54.1 0.6 multiply_reduce_fusion
  54.7 22.0 %all-reduce = (f32[]{:T(128)}, f32[]{:T(128)}) all-reduce(f32[]{:T(128)} %get-tuple-element.12, f32[]{:T(128)} %get-tuple-element.14), channel_id=1, replica_groups=mesh['dp'=8,'tensor'=4] {'dp'}, use_global_device_ids=true, to_apply=%region_12.13 | all-reduce | flops 2 | bytes 16 | tf_op jit(solution)/shard_map/psum | solution.py:101
  77.5 1.6 fusion.3
  79.1 0.0 all-gather.2.cloned.1.call-update
  79.1 0.0 reduce-scatter.2.cloned.1.call-start
  79.2 10.9 %fusion.9 = f32[512,5120]{1,0:T(8,128)} fusion(bf16[512,1024]{1,0:T(8,128)(2,1)} %fusion.3, bf16[5120,1024]{1,0:T(8,128)(2,1)} %param.9), kind=kOutput, calls=%fused_computation.37 | convolution fusion | flops 5368709120 | bytes 22020096 | tf_op jit(solution)/shard_map/dot_general | solution.py:18
  90.1 0.0 reduce-scatter.2.cloned.1.call-update
  90.1 2.0 bitcast_dynamic-update-slice_fusion.7
  92.1 2.0 bitcast_dynamic-update-slice_fusion.6
  94.1 2.1 bitcast_dynamic-update-slice_fusion.5
  96.2 2.2 bitcast_dynamic-update-slice_fusion.4
  98.4 2.2 bitcast_dynamic-update-slice_fusion.3
  100.6 2.2 bitcast_dynamic-update-slice_fusion.2
  102.8 2.1 bitcast_dynamic-update-slice_fusion.1
  104.8 2.0 bitcast_dynamic-update-slice_fusion
  106.9 4.6 %all-to-all-start = ((bf16[8,512,640]{2,1,0:T(8,128)(2,1)}), bf16[8,512,640]{2,1,0:T(8,128)(2,1)}, u32[]{:S(2)}, u32[]{:S(2)}) async-start(bf16[8,512,640]{2,1,0:T(8,128)(2,1)} %bitcast_dynamic-update-slice_fusion), calls=%async_computation.1 | async-start | bytes 10485760 | tf_op jit(solution)/shard_map/all_to_all | solution.py:96
  112.2 191.1 %all-to-all-done = bf16[8,512,640]{2,1,0:T(8,128)(2,1)} async-done(((bf16[8,512,640]{2,1,0:T(8,128)(2,1)}), bf16[8,512,640]{2,1,0:T(8,128)(2,1)}, u32[]{:S(2)}, u32[]{:S(2)}) %all-to-all-start) | async-done | bytes 5242912 | tf_op jit(solution)/shard_map/all_to_all | solution.py:96
  303.3 10.6 %fusion.10 = f32[640,1024]{1,0:T(8,128)} fusion(bf16[4096,640]{1,0:T(8,128)(2,1)} %bitcast.8, bf16[4096,1024]{1,0:T(8,128)(2,1)} %all-gather.2.cloned.1.call-done), kind=kOutput, calls=%fused_computation.38 | convolution fusion | flops 5368709120 | bytes 16252928 | tf_op jit(solution)/shard_map/dot_general | solution.py:12
  (10 shorter events, 0.0 us)
Async XLA Ops:
  8.0 295.3 %all-gather.2.cloned.1.call-start = ((), (), s32[]{:S(2)}) async-start(), calls=%async_computation.3 | async-start | bytes 9437184 | tf_op jit(solution)/shard_map/all_gather | solution.py:99
  30.4 16.4 %copy-start = (s32[512]{0:T(512)S(1)}, s32[512]{0:T(512)}, u32[]{:S(2)}) copy-start(s32[512]{0:T(512)} %param.10) | copy-start | bytes 6148
  30.4 23.7 %copy-start.1 = (f32[512]{0:T(512)S(1)}, f32[512]{0:T(512)}, u32[]{:S(2)}) copy-start(f32[512]{0:T(512)} %param.11) | copy-start | bytes 6148
  79.1 234.8 %reduce-scatter.2.cloned.1.call-start = ((), (), s32[]{:S(2)}) async-start(), calls=%async_computation.2 | async-start | bytes 13107200 | tf_op jit(solution)/shard_map/reduce_scatter | solution.py:100
  106.9 196.4 %all-to-all-start = ((bf16[8,512,640]{2,1,0:T(8,128)(2,1)}), bf16[8,512,640]{2,1,0:T(8,128)(2,1)}, u32[]{:S(2)}, u32[]{:S(2)}) async-start(bf16[8,512,640]{2,1,0:T(8,128)(2,1)} %bitcast_dynamic-update-slice_fusion), calls=%async_computation.1 | async-start | bytes 10485760 | tf_op jit(solution)/shard_map/all_to_all | solution.py:96
Sparse Core Ops, SparseCore 0:
  79.2 216.8 all-gather.1
Sparse Core Ops, SparseCore 1:
  90.2 81.7 reduce-scatter.1
